TPU v7x, 32 devices: a whole 2x2x4 slice. The times are simulated.
32 devices in a mesh: tok: 8 (over z, x), exp: 4 (over y, core).
Axes of the slice: x: 2, y: 2, z: 4, core: 2. Of those that a mesh axis runs over, the one named last changes fastest.
Arguments:
- tokens: bfloat16 [16384, 7168], P('tok', 'exp'), may hold values from -6 to 6
- gate_weight: bfloat16 [7168, 256], P('exp'), may hold values from -0.0625 to 0.0625
- expert_ids: int32 [16384, 8], P('tok'), may hold values from 0 to 255, all different within a row
- expert_bias: float32 [256], P('exp'), may hold values from -0.002 to 0.002
Outputs:
- affinities: float32 [16384, 256], P('tok', 'exp')
- weights: float32 [16384, 8], P('tok')
- load: float32 [256], replicated
- new_bias: float32 [256], replicated
All inputs are finite; a program needn't handle non-finite values.
Results may differ from a plain program's by a relative error of at most 0.0003.
Values may be sent and summed in bfloat16 or wider, within the bound.
No kernel may reach another device: no remote copies, remote signals or barrier semaphores. Data moves between devices by JAX's collectives and lax.ppermute only.
A program may use at most 64 MiB of HBM per device.

v0:
```python
import jax
import jax.numpy as jnp
from jax import lax
from jax.sharding import PartitionSpec as P


def count_experts(expert_ids, width):
    numbers = lax.iota(jnp.int32, width)
    matches = expert_ids[:, :, None] == numbers[None, None, :]
    return jnp.sum(matches.astype(jnp.float32), axis=(0, 1))


def local(tokens, gate_weight, expert_ids, expert_bias):
    experts_all = gate_weight.shape[1]
    own_width = expert_bias.shape[0]
    first_expert = lax.axis_index("exp") * own_width
    tok_rows = tokens.shape[0]
    partial_logits = jnp.dot(tokens, gate_weight, preferred_element_type=jnp.float32)
    logits = lax.psum_scatter(partial_logits, "exp", scatter_dimension=1, tiled=True)
    affinities = jax.nn.sigmoid(logits)
    numbers = first_expert + lax.iota(jnp.int32, own_width)
    matches = expert_ids[:, :, None] == numbers[None, None, :]
    chosen_part = jnp.sum(jnp.where(matches, affinities[:, None, :], jnp.float32(0.0)), axis=2)
    chosen = lax.psum(chosen_part, "exp")
    weights = 2.5 * chosen / jnp.sum(chosen, axis=1, keepdims=True)
    target = jnp.float32(tok_rows * lax.axis_size("tok") * expert_ids.shape[1])
    bias_whole = lax.all_gather(expert_bias, "exp", axis=0, tiled=True)
    load = lax.psum(count_experts(expert_ids, experts_all), "tok")
    new_bias = bias_whole + 0.001 * jnp.sign(target - jnp.float32(experts_all) * load)
    return (affinities, weights, load, new_bias)


def solution(mesh):
    in_specs = (P("tok", "exp"), P("exp", None), P("tok", None), P("exp"))
    out_specs = (P("tok", "exp"), P("tok", None), P(), P())
    return jax.shard_map(local, mesh=mesh, in_specs=in_specs, out_specs=out_specs, check_vma=False)
```

profile of v0, /device:TPU:0, one launch (start us, length us, event | category | flops | bytes accessed | tf_op | source)
XLA Modules:
  0.0 92.7 jit_solution(2102868022089184914)
XLA Ops:
  7.2 0.0 copy-start
  7.2 0.0 copy-start.5
  7.2 0.0 copy-start.2
  7.2 0.0 reduce-scatter.2.cloned.1.call-start
  7.3 1.1 %copy-done = bf16[1792,256]{1,0:T(8,128)(2,1)S(1)} copy-done((bf16[1792,256]{1,0:T(8,128)(2,1)S(1)}, bf16[1792,256]{1,0:T(8,128)(2,1)}, u32[]{:S(2)}) %copy-start) | copy-done | bytes 917528
  8.4 6.5 %fusion = f32[2048,256]{0,1:T(8,128)} fusion(bf16[2048,1792]{1,0:T(8,128)(2,1)} %param.4, bf16[1792,256]{1,0:T(8,128)(2,1)S(1)} %copy-done), kind=kOutput, calls=%fused_computation.7 | convolution fusion | flops 1879048192 | bytes 10354688 | tf_op jit(solution)/shard_map/dot_general | solution.py:18
  14.9 0.0 reduce-scatter.2.cloned.1.call-update
  14.9 0.0 all-reduce.3.cloned.1.call-start
  15.0 0.0 copy-done.2
  15.0 0.3 copy.11
  15.4 0.6 dynamic-slice
  16.6 0.2 dynamic-update-slice
  16.9 5.1 %convert_reduce_fusion = f32[256]{0:T(256)S(1)} fusion(s32[2048,8]{1,0:T(8,128)S(1)} %copy.11), kind=kLoop, calls=%fused_computation | loop fusion | flops 12582656 | bytes 66560 | tf_op jit(solution)/shard_map/reduce_sum | solution.py:10
  22.0 23.1 %psum.15 = f32[256]{0:T(256)S(1)} all-reduce(f32[256]{0:T(256)S(1)} %convert_reduce_fusion), channel_id=1, replica_groups=mesh['tok'=8,'exp'=4] {'tok'}, use_global_device_ids=true, to_apply=%region_5.6 | all-reduce | flops 256 | bytes 2048 | tf_op jit(solution)/shard_map/psum | solution.py:28
  45.1 5.7 %all-reduce = f32[256]{0:T(256)S(1)} all-reduce(f32[256]{0:T(256)S(1)} %dynamic-update-slice), channel_id=1, replica_groups=mesh['tok'=8,'exp'=4] {'exp'}, use_global_device_ids=true, to_apply=%add | all-reduce | flops 256 | bytes 2048
  50.8 0.0 reduce-scatter.2.cloned.1.call-done
  50.8 1.2 %add_divide_fusion = f32[2048,64]{0,1:T(8,128)S(1)} fusion(f32[2048,64]{0,1:T(8,128)} %reduce-scatter.2.cloned.1.call-done), kind=kLoop, calls=%fused_computation.3 | loop fusion | flops 393216 | bytes 1048576 | tf_op jit(solution)/shard_map/div | solution.py:20
  52.0 0.0 copy-start.1
  52.0 1.2 %select_reduce_fusion = f32[2048,8]{0,1:T(8,128)} fusion(f32[2048,64]{0,1:T(8,128)S(1)} %add_divide_fusion, s32[2048,8]{0,1:T(8,128)S(1)} %copy-done.2, s32[64]{0:T(128)S(1)} %iota_add_fusion), kind=kLoop, calls=%fused_computation.2 | loop fusion | flops 3129344 | bytes 655616 | tf_op jit(solution)/shard_map/reduce_sum | solution.py:23
  53.2 0.0 all-reduce.3.cloned.1.call-update
  53.2 0.6 multiply_add_fusion
  53.8 29.7 %all-reduce.3.cloned.1.call-done = f32[2048,8]{0,1:T(8,128)} async-done(((f32[2048,8]{0,1:T(8,128)}), f32[2048,8]{0,1:T(8,128)}) %all-reduce.3.cloned.1.call-update) | async-done | bytes 65552 | tf_op jit(solution)/shard_map/psum | solution.py:24
  83.5 0.9 reduce_sum.28
  84.4 1.5 %multiply_divide_fusion = f32[2048,8]{0,1:T(8,128)} fusion(f32[2048,8]{0,1:T(8,128)} %all-reduce.3.cloned.1.call-done, f32[2048]{0:T(1024)S(1)} %reduce_sum.28), kind=kLoop, calls=%fused_computation.4 | loop fusion | flops 32768 | bytes 139264 | tf_op jit(solution)/shard_map/div | solution.py:25
  (8 shorter events, 0.0 us)
Async XLA Ops:
  7.2 1.2 %copy-start = (bf16[1792,256]{1,0:T(8,128)(2,1)S(1)}, bf16[1792,256]{1,0:T(8,128)(2,1)}, u32[]{:S(2)}) copy-start(bf16[1792,256]{1,0:T(8,128)(2,1)} %param.5) | copy-start | bytes 2752516
  7.2 8.2 %copy-start.5 = (u32[32]{0:T(128)S(1)}, u32[32]{0:T(128)}, u32[]{:S(2)}) copy-start(u32[32]{0:T(128)} %constant.20) | copy-start | bytes 388
  7.2 7.8 %copy-start.2 = (s32[2048,8]{0,1:T(8,128)S(1)}, s32[2048,8]{0,1:T(8,128)}, u32[]{:S(2)}) copy-start(s32[2048,8]{0,1:T(8,128)} %param.6) | copy-start | bytes 196612
  7.2 9.4 %copy-start.4 = (f32[64]{0:T(128)S(1)}, f32[64]{0:T(128)}, u32[]{:S(2)}) copy-start(f32[64]{0:T(128)} %param.7) | copy-start | bytes 772
  7.2 43.6 %reduce-scatter.2.cloned.1.call-start = ((), (), s32[]{:S(2)}) async-start(), calls=%async_computation.1 | async-start | bytes 2621440 | tf_op jit(solution)/shard_map/reduce_scatter | solution.py:19
  14.9 68.6 %all-reduce.3.cloned.1.call-start = ((), (), s32[]{:S(2)}) async-start(), calls=%async_computation.2 | async-start | bytes 131072 | tf_op jit(solution)/shard_map/psum | solution.py:24
  45.1 40.8 %copy-start.3 = (f32[256]{0:T(256)}, f32[256]{0:T(256)S(1)}, u32[]{:S(2)}) copy-start(f32[256]{0:T(256)S(1)} %psum.15) | copy-start | bytes 3076
  52.0 33.9 %copy-start.1 = (f32[2048,64]{0,1:T(8,128)}, f32[2048,64]{0,1:T(8,128)S(1)}, u32[]{:S(2)}) copy-start(f32[2048,64]{0,1:T(8,128)S(1)} %add_divide_fusion) | copy-start | bytes 1572868
Sparse Core Ops, SparseCore 0:
  15.1 33.8 reduce-scatter.1
  53.3 30.1 all-reduce.2
where the time goes:
time: 93.1 us; the launch traced here: 92.7 us
  waiting for transfers between devices  29.8 us (32%)
  blocking collectives  28.8 us (31%)
  between operations  14.8 us (16%)
  other arithmetic  10.4 us (11%)
  matrix products  6.53 us (7%)
  local copies, waits for them, and re-layouts  2.31 us (2%)
    psum x1, waiting for transfers between devices, local(): chosen = lax.psum(chosen_part, 'exp')  29.7 us
    psum x1, blocking collectives, local(): load = lax.psum(count_experts(expert_ids, experts_all), 'tok')  23.1 us
    dot_general x1, matrix products, local(): jnp.dot(tokens, gate_weight, preferred_element_type=jnp.float32)  6.53 us
    unnamed x1, blocking collectives  5.66 us
    reduce_sum x1, other arithmetic, count_experts(): return jnp.sum(matches.astype(jnp.float32), axis=(0, 1))  5.11 us
    unnamed x16, local copies, waits for them, and re-layouts  2.31 us
  transfers between devices with their start and end apart: 2, of which 1 were waited for; matrix products, arithmetic and copies ran while one was open for 7% of the time, Pallas kernels for 0%

commit v1 on v0

--- a/solution.py
+++ b/solution.py
@@ -21,7 +21,9 @@
     numbers = first_expert + lax.iota(jnp.int32, own_width)
     matches = expert_ids[:, :, None] == numbers[None, None, :]
     chosen_part = jnp.sum(jnp.where(matches, affinities[:, None, :], jnp.float32(0.0)), axis=2)
-    chosen = lax.psum(chosen_part, "exp")
+    chosen = chosen_part
+    for hop in (1, 2):
+        chosen = chosen + lax.ppermute(chosen, "exp", [(dev, dev ^ hop) for dev in range(4)])
     weights = 2.5 * chosen / jnp.sum(chosen, axis=1, keepdims=True)
     target = jnp.float32(tok_rows * lax.axis_size("tok") * expert_ids.shape[1])
     bias_whole = lax.all_gather(expert_bias, "exp", axis=0, tiled=True)

time: 93.1 us -> 96.9 us (1.041)
  waiting for transfers between devices: 29.8 us -> 37.2 us
  other arithmetic: 10.4 us -> 8.14 us
  blocking collectives: 28.8 us -> 27.3 us
    reduce_scatter x1, waiting for transfers between devices: 0.01 us -> 33.7 us  [local(): lax.psum_scatter(partial_logits, 'exp', scatter_dimension=1, tiled=True)]
    psum x1 -> x0, waiting for transfers between devices: 29.7 us -> none  [local(): chosen = lax.psum(chosen_part, 'exp')]
    ppermute x0 -> x2, waiting for transfers between devices: none -> 3.42 us  [local(): lax.ppermute(chosen, 'exp', [(dev, dev ^ hop) for dev in range(4)])]
    psum x1, blocking collectives: 23.1 us -> 21.3 us  [local(): load = lax.psum(count_experts(expert_ids, experts_all), 'tok')]
  transfers between devices with their start and end apart: 2 -> 3, of which waited for: 1 -> 2; matrix products, arithmetic and copies ran while one was open for 7% -> 7% of each run, Pallas kernels for 0% -> 0%
where the time goes in v1:
time: 96.9 us; the launch traced here: 96.6 us
  waiting for transfers between devices  37.2 us (38%)
  blocking collectives  27.3 us (28%)
  between operations  14.8 us (15%)
  other arithmetic  8.14 us (8%)
  matrix products  6.54 us (7%)
  local copies, waits for them, and re-layouts  2.3 us (2%)
    reduce_scatter x1, waiting for transfers between devices, local(): lax.psum_scatter(partial_logits, 'exp', scatter_dimension=1, tiled=True)  33.7 us
    psum x1, blocking collectives, local(): load = lax.psum(count_experts(expert_ids, experts_all), 'tok')  21.3 us
    dot_general x1, matrix products, local(): jnp.dot(tokens, gate_weight, preferred_element_type=jnp.float32)  6.54 us
    unnamed x1, blocking collectives  5.96 us
    reduce_sum x1, other arithmetic, count_experts(): return jnp.sum(matches.astype(jnp.float32), axis=(0, 1))  5.12 us
    ppermute x2, waiting for transfers between devices, local(): lax.ppermute(chosen, 'exp', [(dev, dev ^ hop) for dev in range(4)])  3.42 us
    unnamed x16, local copies, waits for them, and re-layouts  2.3 us
  transfers between devices with their start and end apart: 3, of which 2 were waited for; matrix products, arithmetic and copies ran while one was open for 7% of the time, Pallas kernels for 0%

profile of v1, /device:TPU:0, one launch (start us, length us, event | category | flops | bytes accessed | tf_op | source)
XLA Modules:
  0.0 96.6 jit_solution(599852570344160764)
XLA Ops:
  7.2 0.0 copy-start
  7.2 0.0 copy-start.2
  7.2 0.0 reduce-scatter.2.cloned.1.call-start
  7.2 1.1 %copy-done = bf16[1792,256]{1,0:T(8,128)(2,1)S(1)} copy-done((bf16[1792,256]{1,0:T(8,128)(2,1)S(1)}, bf16[1792,256]{1,0:T(8,128)(2,1)}, u32[]{:S(2)}) %copy-start) | copy-done | bytes 917528
  8.4 6.5 %fusion = f32[2048,256]{0,1:T(8,128)} fusion(bf16[2048,1792]{1,0:T(8,128)(2,1)} %param.4, bf16[1792,256]{1,0:T(8,128)(2,1)S(1)} %copy-done), kind=kOutput, calls=%fused_computation.8 | convolution fusion | flops 1879048192 | bytes 10354688 | tf_op jit(solution)/shard_map/dot_general | solution.py:18
  14.9 0.0 reduce-scatter.2.cloned.1.call-update
  14.9 0.3 copy.11
  15.3 33.7 %reduce-scatter.2.cloned.1.call-done = f32[2048,64]{0,1:T(8,128)} async-done(((f32[2048,256]{0,1:T(8,128)}), f32[2048,64]{0,1:T(8,128)}) %reduce-scatter.2.cloned.1.call-update) | async-done | bytes 524304 | tf_op jit(solution)/shard_map/reduce_scatter | solution.py:19
  49.0 1.2 %add_divide_fusion = f32[2048,64]{0,1:T(8,128)S(1)} fusion(f32[2048,64]{0,1:T(8,128)} %reduce-scatter.2.cloned.1.call-done), kind=kLoop, calls=%fused_computation.3 | loop fusion | flops 393216 | bytes 1048576 | tf_op jit(solution)/shard_map/div | solution.py:20
  50.2 0.0 copy-start.1
  50.2 0.6 select_reduce_fusion
  50.8 0.1 collective-permute-start
  50.9 5.1 %convert_reduce_fusion = f32[256]{0:T(256)S(1)} fusion(s32[2048,8]{1,0:T(8,128)S(1)} %copy.11), kind=kLoop, calls=%fused_computation | loop fusion | flops 12582656 | bytes 66560 | tf_op jit(solution)/shard_map/reduce_sum | solution.py:10
  56.0 0.6 dynamic-slice
  57.2 0.0 copy-done.4
  57.3 0.2 dynamic-update-slice
  57.5 21.3 %psum.7 = f32[256]{0:T(256)S(1)} all-reduce(f32[256]{0:T(256)S(1)} %convert_reduce_fusion), channel_id=1, replica_groups=mesh['tok'=8,'exp'=4] {'tok'}, use_global_device_ids=true, to_apply=%region_4.5 | all-reduce | flops 256 | bytes 2048 | tf_op jit(solution)/shard_map/psum | solution.py:30
  78.8 6.0 %all-reduce = f32[256]{0:T(256)S(1)} all-reduce(f32[256]{0:T(256)S(1)} %dynamic-update-slice), channel_id=1, replica_groups=mesh['tok'=8,'exp'=4] {'exp'}, use_global_device_ids=true, to_apply=%add | all-reduce | flops 256 | bytes 2048
  84.8 0.0 collective-permute-done
  84.8 0.3 collective-permute-start.1
  85.1 0.6 multiply_add_fusion
  85.7 3.4 %collective-permute-done.1 = f32[2048,8]{0,1:T(8,128)S(1)} collective-permute-done((f32[2048,8]{0,1:T(8,128)S(1)}, f32[2048,8]{0,1:T(8,128)S(1)}, u32[]{:S(2)}, u32[]{:S(2)}) %collective-permute-start.1) | collective-permute-done | bytes 65568 | tf_op jit(solution)/shard_map/ppermute | solution.py:26
  89.1 0.7 multiply_divide_fusion
  89.8 0.0 copy-done.3
  (10 shorter events, 0.1 us)
Async XLA Ops:
  7.2 1.2 %copy-start = (bf16[1792,256]{1,0:T(8,128)(2,1)S(1)}, bf16[1792,256]{1,0:T(8,128)(2,1)}, u32[]{:S(2)}) copy-start(bf16[1792,256]{1,0:T(8,128)(2,1)} %param.5) | copy-start | bytes 2752516
  7.2 7.7 %copy-start.2 = (s32[2048,8]{0,1:T(8,128)S(1)}, s32[2048,8]{0,1:T(8,128)}, u32[]{:S(2)}) copy-start(s32[2048,8]{0,1:T(8,128)} %param.6) | copy-start | bytes 196612
  7.2 41.8 %reduce-scatter.2.cloned.1.call-start = ((), (), s32[]{:S(2)}) async-start(), calls=%async_computation.1 | async-start | bytes 2621440 | tf_op jit(solution)/shard_map/reduce_scatter | solution.py:19
  14.9 41.1 %copy-start.5 = (u32[32]{0:T(128)S(1)}, u32[32]{0:T(128)}, u32[]{:S(2)}) copy-start(u32[32]{0:T(128)} %constant.20) | copy-start | bytes 388
  14.9 42.4 %copy-start.4 = (f32[64]{0:T(128)S(1)}, f32[64]{0:T(128)}, u32[]{:S(2)}) copy-start(f32[64]{0:T(128)} %param.7) | copy-start | bytes 772
  50.2 39.6 %copy-start.1 = (f32[2048,64]{0,1:T(8,128)}, f32[2048,64]{0,1:T(8,128)S(1)}, u32[]{:S(2)}) copy-start(f32[2048,64]{0,1:T(8,128)S(1)} %add_divide_fusion) | copy-start | bytes 1572868
  50.8 34.0 %collective-permute-start = (f32[2048,8]{0,1:T(8,128)S(1)}, f32[2048,8]{0,1:T(8,128)S(1)}, u32[]{:S(2)}, u32[]{:S(2)}) collective-permute-start(f32[2048,8]{0,1:T(8,128)S(1)} %select_reduce_fusion), channel_id=1, source_target_pairs={{0,1},{1,0},{2,3},{3,2},{4,5},{5,4},{6,7},{7,6},{8,9},{9,8},{10,11... | collective-permute-start | bytes 196616 | tf_op jit(solution)/shard_map/ppermute | solution.py:26
  78.8 11.0 %copy-start.3 = (f32[256]{0:T(256)}, f32[256]{0:T(256)S(1)}, u32[]{:S(2)}) copy-start(f32[256]{0:T(256)S(1)} %psum.7) | copy-start | bytes 3076
  84.8 4.3 %collective-permute-start.1 = (f32[2048,8]{0,1:T(8,128)S(1)}, f32[2048,8]{0,1:T(8,128)S(1)}, u32[]{:S(2)}, u32[]{:S(2)}) collective-permute-start(f32[2048,8]{0,1:T(8,128)S(1)} %add.29), channel_id=1, source_target_pairs={{0,2},{1,3},{2,0},{3,1},{4,6},{5,7},{6,4},{7,5},{8,10},{9,11},{10,... | collective-permute-start | bytes 196616 | tf_op jit(solution)/shard_map/ppermute | solution.py:26
Sparse Core Ops, SparseCore 0:
  15.0 33.9 reduce-scatter.1
